TPU v7x, 32 devices: a whole 2x2x4 slice. The times are simulated.
32 devices in a mesh: dp: 4 (over z), seq: 8 (over y, x, core).
Axes of the slice: x: 2, y: 2, z: 4, core: 2. Of those that a mesh axis runs over, the one named last changes fastest.
Arguments:
- queries: bfloat16 [4, 2048, 512], P('dp', 'seq'), may hold values from -0.890625 to 0.890625
- keys: bfloat16 [4, 2048, 512], P('dp', 'seq'), may hold values from -0.890625 to 0.890625
- values: bfloat16 [4, 2048, 512], P('dp', 'seq'), may hold values from -6 to 6
- level_weights: float32 [4, 6, 4, 2048], P('dp', None, None, 'seq'), may hold values from 0.25 to 4
- proj: bfloat16 [512, 2048], P(None, 'seq'), may hold values from -0.25 to 0.25
- out_grad: bfloat16 [4, 2048, 2048], P('dp', 'seq'), may hold values from -0.59765625 to 0.59765625
Outputs:
- attended_out: bfloat16 [4, 2048, 2048], P('dp', 'seq')
- grad_queries: bfloat16 [4, 2048, 512], P('dp', 'seq')
- grad_keys: bfloat16 [4, 2048, 512], P('dp', 'seq')
- grad_values: bfloat16 [4, 2048, 512], P('dp', 'seq')
- grad_levels: float32 [4, 6, 4, 2048], P('dp', None, None, 'seq')
- grad_proj: float32 [512, 2048], P(None, 'seq')
All inputs are finite; a program needn't handle non-finite values.
Results may differ from a plain program's by a relative error of at most 0.0064.
Values may be sent and summed in bfloat16 or wider, within the bound.
No kernel may reach another device: no remote copies, remote signals or barrier semaphores. Data moves between devices by JAX's collectives and lax.ppermute only.
A program may use at most 64 MiB of HBM per device.

v0:
```python
import jax
import jax.numpy as jnp
from jax import lax
from jax.sharding import PartitionSpec as P


def partner_2(value, axis, stride):
    mask = 2**stride
    pairs = [(source, source ^ mask) for source in range(lax.axis_size(axis))]
    return lax.ppermute(value, axis, pairs)


def level_table(length, stretch, local_bits):
    place = lax.iota(jnp.int32, length)
    blocks = place // stretch
    apart = jnp.bitwise_xor(blocks[:, None], blocks[None, :])
    table = jnp.zeros((length, length), jnp.int32)
    for bit in range(local_bits):
        table = table + (apart >= 1 << bit).astype(jnp.int32)
    causal = place[:, None] >= place[None, :]
    return (table, causal)


def local_weights(lam, table, causal, local_bits):
    weights = jnp.zeros((lam.shape[1], table.shape[0], table.shape[1]), jnp.float32)
    for level in range(local_bits + 1):
        weights = weights + jnp.where(table[None] == level, lam[level][:, :, None], jnp.float32(0))
    return jnp.where(causal[None], weights, jnp.float32(0))


def marked_bit(index, bit):
    return jnp.bitwise_and(jnp.right_shift(index, bit), 1).astype(jnp.float32)


def shards(queries, keys, values, level_weights, proj, out_grad):
    tokens_here = queries.shape[1]
    heads = level_weights.shape[2]
    levels = level_weights.shape[1]
    width = queries.shape[2]
    size = width // heads
    scale = size ** (-0.5)
    span_count = lax.axis_size("seq")
    dev_bits = span_count.bit_length() - 1
    local_bits = levels - 1 - dev_bits
    stretch = tokens_here >> local_bits
    index = lax.axis_index("seq")
    shape = (tokens_here, heads, size)
    query = queries[0].reshape(shape)
    key = keys[0].reshape(shape)
    value = values[0].reshape(shape)
    lam = level_weights[0]
    grad_out = out_grad[0]
    table, causal = level_table(tokens_here, stretch, local_bits)
    scores = jnp.einsum("thd,shd->hts", query, key, preferred_element_type=jnp.float32)
    weights = local_weights(lam, table, causal, local_bits)
    probs = (scale * weights * scores).astype(jnp.bfloat16)
    total = jnp.einsum("hts,shd->thd", probs, value, preferred_element_type=jnp.float32)
    totals = jnp.einsum("shi,shj->hij", key, value, preferred_element_type=jnp.float32)
    running = totals
    states = []
    for bit in range(dev_bits):
        partner = partner_2(running, "seq", bit)
        states.append((marked_bit(index, bit) * partner).astype(jnp.bfloat16))
        running = running + partner
    cross = jnp.zeros_like(total)
    mapped = []
    for bit in range(dev_bits):
        image = jnp.einsum("thi,hij->thj", query, states[bit], preferred_element_type=jnp.float32)
        mapped.append(image)
        cross = cross + lam[local_bits + 1 + bit].T[:, :, None] * image
    attended = (total + scale * cross).astype(jnp.bfloat16).reshape(tokens_here, width)
    full_proj = lax.all_gather(proj, "seq", axis=1, tiled=True)
    out = jnp.dot(attended, full_proj, preferred_element_type=jnp.float32).astype(jnp.bfloat16)
    grad_att = lax.dot_general(
        grad_out, full_proj, (((1,), (1,)), ((), ())), preferred_element_type=jnp.float32
    ).astype(jnp.bfloat16)
    grad_heads = grad_att.reshape(shape)
    dprob = jnp.einsum("thd,shd->hts", grad_heads, value, preferred_element_type=jnp.float32)
    product = jnp.where(causal[None], scale * scores * dprob, jnp.float32(0))
    grads = [
        jnp.sum(jnp.where(table[None] == level, product, jnp.float32(0)), axis=2)
        for level in range(local_bits + 1)
    ]
    dscore = (scale * weights * dprob).astype(jnp.bfloat16)
    grad_q = jnp.einsum("hts,shd->thd", dscore, key, preferred_element_type=jnp.float32)
    grad_k = jnp.einsum("hts,thd->shd", dscore, query, preferred_element_type=jnp.float32)
    grad_v = jnp.einsum("hts,thd->shd", probs, grad_heads, preferred_element_type=jnp.float32)
    updates = []
    for bit in range(dev_bits):
        grads.append(scale * jnp.sum(grad_heads.astype(jnp.float32) * mapped[bit], axis=2).T)
        weighted = (
            scale * lam[local_bits + 1 + bit].T[:, :, None] * grad_heads.astype(jnp.float32)
        ).astype(jnp.bfloat16)
        updates.append(
            jnp.einsum("thi,thj->hij", query, weighted, preferred_element_type=jnp.float32)
        )
        grad_q = grad_q + jnp.einsum(
            "thj,hij->thi", weighted, states[bit], preferred_element_type=jnp.float32
        )
    pending = [marked_bit(index, bit) * updates[bit] for bit in range(dev_bits)]
    carried = jnp.zeros_like(totals)
    for bit in range(dev_bits):
        sending = jnp.stack(pending[bit:])
        arrived = partner_2(sending, "seq", bit)
        carried = carried + (1.0 - marked_bit(index, bit)) * arrived[0]
        for later in range(bit + 1, dev_bits):
            pending[later] = pending[later] + arrived[later - bit]
    returned = carried.astype(jnp.bfloat16)
    grad_k = grad_k + jnp.einsum(
        "shj,hij->shi", value, returned, preferred_element_type=jnp.float32
    )
    grad_v = grad_v + jnp.einsum("shi,hij->shj", key, returned, preferred_element_type=jnp.float32)
    shard = lax.psum_scatter(
        lax.dot_general(
            grad_out, attended, (((0,), (0,)), ((), ())), preferred_element_type=jnp.float32
        ),
        "seq",
        scatter_dimension=0,
        tiled=True,
    )
    shard = lax.psum(shard, "dp")
    grad_levels = jnp.stack(grads)[None]
    return (
        out[None],
        grad_q.astype(jnp.bfloat16).reshape(1, tokens_here, width),
        grad_k.astype(jnp.bfloat16).reshape(1, tokens_here, width),
        grad_v.astype(jnp.bfloat16).reshape(1, tokens_here, width),
        grad_levels,
        shard.T,
    )


def solution(mesh):
    return jax.shard_map(
        shards,
        mesh=mesh,
        in_specs=(
            P("dp", "seq", None),
            P("dp", "seq", None),
            P("dp", "seq", None),
            P("dp", None, None, "seq"),
            P(None, "seq"),
            P("dp", "seq", None),
        ),
        out_specs=(
            P("dp", "seq", None),
            P("dp", "seq", None),
            P("dp", "seq", None),
            P("dp", "seq", None),
            P("dp", None, None, "seq"),
            P(None, "seq"),
        ),
        check_vma=False,
    )
```

profile of v0, /device:TPU:0, one launch (start us, length us, event | category | flops | bytes accessed | tf_op | source)
XLA Modules:
  0.0 157.5 jit_solution(11511535724584984246)
XLA Ops:
  7.2 0.7 all-gather.2.cloned.1.call-update
  8.0 1.0 reshape_squeeze.10
  9.2 1.1 reshape_squeeze.11
  10.3 0.2 fusion.43
  10.5 0.6 collective-permute-start
  11.2 0.6 slice_bitcast_fusion.8
  11.8 0.9 fusion.29
  12.7 1.3 fusion.31
  14.0 2.6 %collective-permute-start.1 = (f32[4,128,128]{2,1,0:T(8,128)S(1)}, f32[4,128,128]{2,1,0:T(8,128)S(1)}, u32[]{:S(2)}, u32[]{:S(2)}) collective-permute-start(f32[4,128,128]{2,1,0:T(8,128)S(1)} %add.93), channel_id=1, source_target_pairs={{0,2},{1,3},{2,0},{3,1},{4,6},{5,7},{6,4},{7,5},{8,10},{9,11},{10,... | collective-permute-start | bytes 786440 | tf_op jit(solution)/shard_map/ppermute | solution.py:10
  16.5 0.6 iota_compare_fusion
  17.2 0.3 convolution_bitcast_fusion.10
  17.4 8.0 %collective-permute-done.1 = f32[4,128,128]{2,1,0:T(8,128)S(1)} collective-permute-done((f32[4,128,128]{2,1,0:T(8,128)S(1)}, f32[4,128,128]{2,1,0:T(8,128)S(1)}, u32[]{:S(2)}, u32[]{:S(2)}) %collective-permute-start.1) | collective-permute-done | bytes 262176 | tf_op jit(solution)/shard_map/ppermute | solution.py:10
  25.4 0.7 add.95
  26.1 1.4 collective-permute-start.2
  27.5 1.1 convolution_bitcast_fusion.9
  28.6 14.4 %all-gather.2.cloned.1.call-done = bf16[512,2048]{1,0:T(8,128)(2,1)} async-done(((bf16[512,256]{1,0:T(8,128)(2,1)}), bf16[512,2048]{1,0:T(8,128)(2,1)}) %all-gather.2.cloned.1.call-update) | async-done | bytes 2097168 | tf_op jit(solution)/shard_map/all_gather | solution.py:72
  42.9 3.0 %convolution_convert_fusion.1 = bf16[256,512]{1,0:T(8,128)(2,1)} fusion(bf16[512,2048]{1,0:T(8,128)(2,1)} %all-gather.2.cloned.1.call-done, bf16[1,256,2048]{2,1,0:T(8,128)(2,1)S(1)} %copy-done), kind=kOutput, calls=%fused_computation.21 | convolution fusion | flops 537001984 | bytes 3407872 | tf_op jit(solution)/shard_map/dot_general | solution.py:74
  46.0 1.1 copy.24
  47.2 1.5 fusion.18
  48.8 0.7 fusion.7
  49.4 2.7 %convolution_bitcast_fusion = f32[2048,512]{0,1:T(8,128)} fusion(bf16[256,512]{0,1:T(8,128)(2,1)S(1)} %bitcast.163, bf16[1,256,2048]{2,1,0:T(8,128)(2,1)S(1)} %copy-done), kind=kOutput, calls=%fused_computation | convolution fusion | flops 536870912 | bytes 5505024 | tf_op jit(solution)/shard_map/dot_general | solution.py:114
  52.2 0.6 copy-done.20
  52.8 0.2 fusion.10
  53.1 0.2 convolution_multiply_fusion
  53.3 0.2 convolution_multiply_fusion.1
  53.6 0.3 collective-permute-start.3
  54.1 0.7 select_reduce_fusion
  54.8 0.2 convolution_bitcast_fusion.5
  55.1 0.6 convolution_bitcast_fusion.1
  55.9 0.6 convolution_bitcast_fusion.4
  56.5 1.5 fusion.55
  58.1 1.5 collective-permute-start.4
  59.6 0.2 convolution_bitcast_fusion.6
  59.9 0.2 fusion.6
  60.1 12.2 %collective-permute-done.4 = f32[2,4,128,128]{2,3,1,0:T(8,128)S(1)} collective-permute-done((f32[2,4,128,128]{2,3,1,0:T(8,128)S(1)}, f32[2,4,128,128]{2,3,1,0:T(8,128)S(1)}, u32[]{:S(2)}, u32[]{:S(2)}) %collective-permute-start.4) | collective-permute-done | bytes 524320 | tf_op jit(solution)/shard_map/ppermute | solution.py:10
  72.3 0.8 fusion.20
  73.1 1.1 collective-permute-start.5
  74.3 0.6 copy-done.28
  74.9 0.8 copy.41
  75.7 3.3 %fusion = bf16[1,256,2048]{2,1,0:T(8,128)(2,1)} fusion(bf16[256,512]{0,1:T(8,128)(2,1)S(1)} %bitcast.164, bf16[512,2048]{1,0:T(8,128)(2,1)} %all-gather.2.cloned.1.call-done), kind=kOutput, calls=%fused_computation.2 | convolution fusion | flops 537395200 | bytes 3407872 | tf_op jit(solution)/shard_map/dot_general | solution.py:73
  79.1 29.1 %reduce-scatter.2.cloned.1.call-done = f32[256,512]{0,1:T(8,128)} async-done(((f32[2048,512]{0,1:T(8,128)}), f32[256,512]{0,1:T(8,128)}) %reduce-scatter.2.cloned.1.call-update) | async-done | bytes 524304 | tf_op jit(solution)/shard_map/reduce_scatter | solution.py:113
  108.2 1.1 fusion.45
  109.3 0.3 fusion.9
  109.6 0.8 copy.42
  110.4 0.2 fusion.8
  110.6 0.8 copy.43
  111.5 37.6 %all-reduce.2.cloned.1.call-done = f32[512,256]{1,0:T(8,128)} async-done(((f32[512,256]{1,0:T(8,128)}), f32[512,256]{1,0:T(8,128)}) %all-reduce.2.cloned.1.call-update) | async-done | bytes 524304 | tf_op jit(solution)/shard_map/psum | solution.py:121
  149.1 1.9 %copy.96 = f32[512,256]{1,0:T(8,128)} copy(f32[512,256]{1,0:T(8,128)} %all-reduce.2.cloned.1.call-done) | data formatting | bytes 1048576
  (79 shorter events, 1.1 us)
Async XLA Ops:
  7.2 35.8 %copy-start = (bf16[1,256,2048]{2,1,0:T(8,128)(2,1)S(1)}, bf16[1,256,2048]{2,1,0:T(8,128)(2,1)}, u32[]{:S(2)}) copy-start(bf16[1,256,2048]{2,1,0:T(8,128)(2,1)} %param.11) | copy-start | bytes 3145732
  7.2 3.9 %copy-start.12 = (bf16[1,256,512]{2,1,0:T(8,128)(2,1)S(1)}, bf16[1,256,512]{2,1,0:T(8,128)(2,1)}, u32[]{:S(2)}) copy-start(bf16[1,256,512]{2,1,0:T(8,128)(2,1)} %param.6) | copy-start | bytes 786436
  7.2 4.0 %copy-start.19 = (f32[1,6,4,256]{3,2,1,0:T(4,128)S(1)}, f32[1,6,4,256]{3,2,1,0:T(4,128)}, u32[]{:S(2)}) copy-start(f32[1,6,4,256]{3,2,1,0:T(4,128)} %param.9) | copy-start | bytes 73732
  7.2 35.7 %all-gather.2.cloned.1.call-start = ((), (), s32[]{:S(2)}) async-start(), calls=%async_computation.1 | async-start | bytes 2359296 | tf_op jit(solution)/shard_map/all_gather | solution.py:72
  7.9 100.2 %reduce-scatter.2.cloned.1.call-start = ((), (), s32[]{:S(2)}) async-start(), calls=%async_computation.2 | async-start | bytes 4718592 | tf_op jit(solution)/shard_map/reduce_scatter | solution.py:113
  9.2 1.1 copy-start.3
  10.5 3.4 %collective-permute-start = (f32[4,128,128]{2,1,0:T(8,128)S(1)}, f32[4,128,128]{2,1,0:T(8,128)S(1)}, u32[]{:S(2)}, u32[]{:S(2)}) collective-permute-start(f32[4,128,128]{2,1,0:T(8,128)S(1)} %fusion.43), channel_id=1, source_target_pairs={{0,1},{1,0},{2,3},{3,2},{4,5},{5,4},{6,7},{7,6},{8,9},{9,8},{10,11... | collective-permute-start | bytes 786440 | tf_op jit(solution)/shard_map/ppermute | solution.py:10
  14.0 11.4 %collective-permute-start.1 = (f32[4,128,128]{2,1,0:T(8,128)S(1)}, f32[4,128,128]{2,1,0:T(8,128)S(1)}, u32[]{:S(2)}, u32[]{:S(2)}) collective-permute-start(f32[4,128,128]{2,1,0:T(8,128)S(1)} %add.93), channel_id=1, source_target_pairs={{0,2},{1,3},{2,0},{3,1},{4,6},{5,7},{6,4},{7,5},{8,10},{9,11},{10,... | collective-permute-start | bytes 786440 | tf_op jit(solution)/shard_map/ppermute | solution.py:10
  26.1 21.0 %collective-permute-start.2 = (f32[4,128,128]{2,1,0:T(8,128)}, f32[4,128,128]{2,1,0:T(8,128)S(1)}, u32[]{:S(2)}, u32[]{:S(2)}) collective-permute-start(f32[4,128,128]{2,1,0:T(8,128)} %add.95), channel_id=1, source_target_pairs={{0,4},{1,5},{2,6},{3,7},{4,0},{5,1},{6,2},{7,3},{8,12},{9,13},{10,... | collective-permute-start | bytes 786440 | tf_op jit(solution)/shard_map/ppermute | solution.py:10
  47.1 1.6 %copy-start.1 = (f32[256,4,128]{0,2,1:T(8,128)S(1)}, f32[256,4,128]{0,2,1:T(8,128)}, u32[]{:S(2)}) copy-start(f32[256,4,128]{0,2,1:T(8,128)} %convolution_bitcast_fusion.9) | copy-start | bytes 1572868
  47.1 1.6 %copy-start.5 = (f32[4,256,256]{1,2,0:T(8,128)S(1)}, f32[4,256,256]{1,2,0:T(8,128)}, u32[]{:S(2)}) copy-start(f32[4,256,256]{1,2,0:T(8,128)} %fusion.31) | copy-start | bytes 3145732
  47.1 1.6 %copy-start.13 = (pred[256,256]{0,1:T(8,128)(4,1)S(1)}, pred[256,256]{0,1:T(8,128)(4,1)}, u32[]{:S(2)}) copy-start(pred[256,256]{0,1:T(8,128)(4,1)} %get-tuple-element.31) | copy-start | bytes 196612
  47.1 1.6 %copy-start.16 = (pred[256,256]{0,1:T(8,128)(4,1)S(1)}, pred[256,256]{0,1:T(8,128)(4,1)}, u32[]{:S(2)}) copy-start(pred[256,256]{0,1:T(8,128)(4,1)} %iota_compare_fusion) | copy-start | bytes 196612
  47.1 1.6 %copy-start.21 = (f32[4,256]{1,0:T(4,128)S(1)}, f32[4,256]{1,0:T(4,128)}, u32[]{:S(2)}) copy-start(f32[4,256]{1,0:T(4,128)} %get-tuple-element.25) | copy-start | bytes 12292
  47.1 1.6 %copy-start.23 = (f32[4,256]{1,0:T(4,128)S(1)}, f32[4,256]{1,0:T(4,128)}, u32[]{:S(2)}) copy-start(f32[4,256]{1,0:T(4,128)} %get-tuple-element.26) | copy-start | bytes 12292
  47.1 1.6 %copy-start.25 = (f32[256,4]{0,1:T(4,128)S(1)}, f32[256,4]{0,1:T(4,128)}, u32[]{:S(2)}) copy-start(f32[256,4]{0,1:T(4,128)} %get-tuple-element.24) | copy-start | bytes 12292
  47.1 1.6 %copy-start.26 = (f32[256,4]{0,1:T(4,128)S(1)}, f32[256,4]{0,1:T(4,128)}, u32[]{:S(2)}) copy-start(f32[256,4]{0,1:T(4,128)} %get-tuple-element.27) | copy-start | bytes 12292
  47.1 1.6 %copy-start.27 = (f32[256,4]{0,1:T(4,128)S(1)}, f32[256,4]{0,1:T(4,128)}, u32[]{:S(2)}) copy-start(f32[256,4]{0,1:T(4,128)} %get-tuple-element.28) | copy-start | bytes 12292
  47.2 1.5 copy-start.7
  52.1 0.7 copy-start.20
  52.1 1.8 %copy-start.14 = (pred[256,256]{0,1:T(8,128)(4,1)S(1)}, pred[256,256]{0,1:T(8,128)(4,1)}, u32[]{:S(2)}) copy-start(pred[256,256]{0,1:T(8,128)(4,1)} %get-tuple-element.31) | copy-start | bytes 196612
  52.1 1.8 %copy-start.17 = (pred[256,256]{0,1:T(8,128)(4,1)S(1)}, pred[256,256]{0,1:T(8,128)(4,1)}, u32[]{:S(2)}) copy-start(pred[256,256]{0,1:T(8,128)(4,1)} %iota_compare_fusion) | copy-start | bytes 196612
  52.1 96.9 %all-reduce.2.cloned.1.call-start = ((), (), s32[]{:S(2)}) async-start(), calls=%async_computation.3 | async-start | bytes 1048576 | tf_op jit(solution)/shard_map/psum | solution.py:121
  52.8 1.2 copy-start.6
  53.6 1.2 copy-start.8
  53.6 1.4 copy-start.4
  53.6 1.4 copy-start.22
  53.6 1.4 copy-start.24
  53.6 4.4 %collective-permute-start.3 = (f32[3,4,128,128]{2,3,1,0:T(8,128)S(1)}, f32[3,4,128,128]{2,3,1,0:T(8,128)S(1)}, u32[]{:S(2)}, u32[]{:S(2)}) collective-permute-start(f32[3,4,128,128]{2,3,1,0:T(8,128)S(1)} %pad_maximum_fusion), channel_id=1, source_target_pairs={{0,1},{1,0},{2,3},{3,2},{4,5},{5,4},{6,7},{7,6},{8,9},{9,8},{10,11... | collective-permute-start | bytes 2359304 | tf_op jit(solution)/shard_map/ppermute | solution.py:10
  55.0 0.8 copy-start.15
  55.0 0.9 copy-start.18
  58.0 14.2 %copy-start.2 = (f32[3,4,128,128]{2,3,1,0:T(8,128)}, f32[3,4,128,128]{2,3,1,0:T(8,128)S(1)}, u32[]{:S(2)}) copy-start(f32[3,4,128,128]{2,3,1,0:T(8,128)S(1)} %collective-permute-done.3) | copy-start | bytes 2359300
  58.1 14.1 %collective-permute-start.4 = (f32[2,4,128,128]{2,3,1,0:T(8,128)S(1)}, f32[2,4,128,128]{2,3,1,0:T(8,128)S(1)}, u32[]{:S(2)}, u32[]{:S(2)}) collective-permute-start(f32[2,4,128,128]{2,3,1,0:T(8,128)S(1)} %pad_maximum_fusion.1), channel_id=1, source_target_pairs={{0,2},{1,3},{2,0},{3,1},{4,6},{5,7},{6,4},{7,5},{8,10},{9,11},{10,... | collective-permute-start | bytes 1572872 | tf_op jit(solution)/shard_map/ppermute | solution.py:10
  72.3 0.9 copy-start.10
  73.1 35.0 %collective-permute-start.5 = (f32[1,4,128,128]{2,3,1,0:T(8,128)}, f32[1,4,128,128]{2,3,1,0:T(8,128)}, u32[]{:S(2)}, u32[]{:S(2)}) collective-permute-start(f32[1,4,128,128]{2,3,1,0:T(8,128)} %fusion.20), channel_id=1, source_target_pairs={{0,4},{1,5},{2,6},{3,7},{4,0},{5,1},{6,2},{7,3},{8,12},{9,13},{10,... | collective-permute-start | bytes 786440 | tf_op jit(solution)/shard_map/ppermute | solution.py:10
  74.3 0.6 copy-start.28
  75.7 32.5 %copy-start.11 = (f32[2,4,128,128]{2,3,1,0:T(8,128)S(1)}, f32[2,4,128,128]{2,3,1,0:T(8,128)}, u32[]{:S(2)}) copy-start(f32[2,4,128,128]{2,3,1,0:T(8,128)} %copy-done.10) | copy-start | bytes 1572868
  79.1 31.3 %copy-start.9 = (f32[4,128,256]{2,1,0:T(8,128)S(1)}, f32[4,128,256]{2,1,0:T(8,128)}, u32[]{:S(2)}) copy-start(f32[4,128,256]{2,1,0:T(8,128)} %fusion.55) | copy-start | bytes 1572868
Sparse Core Ops, SparseCore 0:
  9.9 32.9 all-gather.1
  52.2 55.8 reduce-scatter.1
  110.5 38.5 all-reduce.1
where the time goes:
time: 158 us; the launch traced here: 157 us
  waiting for transfers between devices  102 us (65%)
  matrix products  19.2 us (12%)
  between operations  14.2 us (9%)
  local copies, waits for them, and re-layouts  10.2 us (6%)
  starting transfers between devices  7.56 us (5%)
  other arithmetic  4.34 us (3%)
    psum x1, waiting for transfers between devices, shards(): shard = lax.psum(shard, 'dp')  37.6 us
    reduce_scatter x1, waiting for transfers between devices, shards(): lax.psum_scatter(lax.dot_general(grad_out, attended, (((0,), (0,)), ((),...  29.1 us
    ppermute x6, waiting for transfers between devices, partner_2(): return lax.ppermute(value, axis, pairs)  20.1 us
    all_gather x1, waiting for transfers between devices, shards(): full_proj = lax.all_gather(proj, 'seq', axis=1, tiled=True)  14.4 us
    ppermute x6, starting transfers between devices, partner_2(): return lax.ppermute(value, axis, pairs)  7.44 us
    unnamed x65, local copies, waits for them, and re-layouts  6.16 us
    dot_general x1, matrix products, shards(): jnp.dot(attended, full_proj, preferred_element_type=jnp.float32)  3.35 us
  transfers between devices with their start and end apart: 9, of which 5 were waited for; matrix products, arithmetic and copies ran while one was open for 16% of the time, Pallas kernels for 0%

commit v1 on v0

--- a/solution.py
+++ b/solution.py
@@ -69,7 +69,7 @@
         mapped.append(image)
         cross = cross + lam[local_bits + 1 + bit].T[:, :, None] * image
     attended = (total + scale * cross).astype(jnp.bfloat16).reshape(tokens_here, width)
-    full_proj = lax.all_gather(proj, "seq", axis=1, tiled=True)
+    full_proj = jnp.concatenate(lax.all_gather(proj, "seq"), axis=1)
     out = jnp.dot(attended, full_proj, preferred_element_type=jnp.float32).astype(jnp.bfloat16)
     grad_att = lax.dot_general(
         grad_out, full_proj, (((1,), (1,)), ((), ())), preferred_element_type=jnp.float32

time: 158 us -> 163 us (1.032)
  local copies, waits for them, and re-layouts: 10.2 us -> 15.4 us
  waiting for transfers between devices: 102 us -> 98.4 us
  matrix products: 19.2 us -> 22.5 us
    reshape x0 -> x1, local copies, waits for them, and re-layouts: none -> 2.86 us  [shards(): full_proj = jnp.concatenate(lax.all_gather(proj, 'seq'), axis=1)]
    unnamed x65 -> x61, local copies, waits for them, and re-layouts: 6.16 us -> 8.37 us
    dot_general x1, matrix products: 3.05 us -> 1.41 us  [shards(): lax.dot_general(grad_out, full_proj, (((1,), (1,)), ((), ())), preferred_...]
  transfers between devices with their start and end apart: 9 -> 9, of which waited for: 5 -> 5; matrix products, arithmetic and copies ran while one was open for 16% -> 19% of each run, Pallas kernels for 0% -> 0%
where the time goes in v1:
time: 163 us; the launch traced here: 162 us
  waiting for transfers between devices  98.4 us (60%)
  matrix products  22.5 us (14%)
  local copies, waits for them, and re-layouts  15.4 us (9%)
  between operations  14.2 us (9%)
  starting transfers between devices  7.94 us (5%)
  other arithmetic  3.56 us (2%)
    psum x1, waiting for transfers between devices, shards(): shard = lax.psum(shard, 'dp')  36.8 us
    reduce_scatter x1, waiting for transfers between devices, shards(): lax.psum_scatter(lax.dot_general(grad_out, attended, (((0,), (0,)), ((),...  28 us
    ppermute x6, waiting for transfers between devices, partner_2(): return lax.ppermute(value, axis, pairs)  19.5 us
    all_gather x1, waiting for transfers between devices, shards(): full_proj = jnp.concatenate(lax.all_gather(proj, 'seq'), axis=1)  13.5 us
    unnamed x61, local copies, waits for them, and re-layouts  8.37 us
    ppermute x6, starting transfers between devices, partner_2(): return lax.ppermute(value, axis, pairs)  7.82 us
    dot_general x3, matrix products, shards(): jnp.einsum('thi,hij->thj', query, states[bit], preferred_element_type=jnp...  3.8 us
    dot_general x1, matrix products, shards(): jnp.dot(attended, full_proj, preferred_element_type=jnp.float32)  3.32 us
  transfers between devices with their start and end apart: 9, of which 5 were waited for; matrix products, arithmetic and copies ran while one was open for 19% of the time, Pallas kernels for 0%

profile of v1, /device:TPU:0, one launch (start us, length us, event | category | flops | bytes accessed | tf_op | source)
XLA Modules:
  0.0 162.0 jit_solution(16712970788787160504)
XLA Ops:
  7.2 0.7 all-gather.3.cloned.1.call-update
  8.0 1.0 reshape_squeeze.10
  9.2 1.1 reshape_squeeze.11
  10.6 0.5 copy-done.4
  11.0 0.5 collective-permute-start
  11.6 0.6 slice_bitcast_fusion.8
  12.2 0.8 fusion.29
  13.1 1.3 fusion.31
  14.4 2.5 %collective-permute-start.1 = (f32[4,128,128]{2,1,0:T(8,128)S(1)}, f32[4,128,128]{2,1,0:T(8,128)S(1)}, u32[]{:S(2)}, u32[]{:S(2)}) collective-permute-start(f32[4,128,128]{2,1,0:T(8,128)S(1)} %add.93), channel_id=1, source_target_pairs={{0,2},{1,3},{2,0},{3,1},{4,6},{5,7},{6,4},{7,5},{8,10},{9,11},{10,... | collective-permute-start | bytes 786440 | tf_op jit(solution)/shard_map/ppermute | solution.py:10
  16.9 0.7 iota_compare_fusion
  17.6 1.1 convolution_bitcast_fusion.10
  18.7 7.3 %collective-permute-done.1 = f32[4,128,128]{2,1,0:T(8,128)S(1)} collective-permute-done((f32[4,128,128]{2,1,0:T(8,128)S(1)}, f32[4,128,128]{2,1,0:T(8,128)S(1)}, u32[]{:S(2)}, u32[]{:S(2)}) %collective-permute-start.1) | collective-permute-done | bytes 262176 | tf_op jit(solution)/shard_map/ppermute | solution.py:10
  26.0 0.8 add.95
  26.8 1.6 collective-permute-start.2
  28.4 1.1 convolution_bitcast_fusion.9
  29.4 13.5 %all-gather.3.cloned.1.call-done = bf16[4096,256]{1,0:T(8,128)(2,1)} async-done(((bf16[512,256]{1,0:T(8,128)(2,1)}), bf16[4096,256]{1,0:T(8,128)(2,1)}) %all-gather.3.cloned.1.call-update) | async-done | bytes 2097168 | tf_op jit(solution)/shard_map/all_gather | solution.py:72
  42.9 2.9 %copy.88 = bf16[512,8,256]{0,2,1:T(8,128)(2,1)S(1)} copy(bf16[512,8,256]{2,0,1:T(8,128)(2,1)} %bitcast.169) | data formatting | bytes 4194304 | tf_op jit(solution)/shard_map/reshape | solution.py:72
  45.8 1.3 copy-done.1
  47.1 1.4 convolution_convert_fusion.1
  48.6 1.2 copy.89
  49.8 1.7 %fusion.18 = (f32[256,4]{0,1:T(4,128)S(1)}, f32[256,4]{0,1:T(4,128)S(1)}, f32[256,4]{0,1:T(4,128)S(1)}, f32[256,4,128]{0,2,1:T(8,128)S(1)}) fusion(bf16[256,512]{0,1:T(8,128)(2,1)S(1)} %copy.89, f32[256,4,128]{0,2,1:T(8,128)} %convolution_bitcast_fusion.9, f32[256,4,128]{0,2,1:T(8,128)} %convolution_bitcast_fusion.10, ...), kind=kOutput, calls=%fused_computation.49 | convolution fusion | flops 34599936 | bytes 2371588 | tf_op jit(solution)/shard_map/thi,hij->thj/dot_general | solution.py:68
  51.5 0.7 fusion.7
  52.2 2.7 %convolution_bitcast_fusion = f32[2048,512]{0,1:T(8,128)} fusion(bf16[256,512]{0,1:T(8,128)(2,1)S(1)} %bitcast.170, bf16[1,256,2048]{2,1,0:T(8,128)(2,1)S(1)} %copy-done), kind=kOutput, calls=%fused_computation | convolution fusion | flops 536870912 | bytes 5505024 | tf_op jit(solution)/shard_map/dot_general | solution.py:114
  54.9 0.7 copy-done.22
  55.8 0.2 convolution_multiply_fusion
  56.4 0.3 collective-permute-start.3
  56.7 1.9 %select_reduce_fusion = (f32[4,256]{1,0:T(4,128)S(1)}, f32[4,256]{1,0:T(4,128)S(1)}, f32[4,256]{1,0:T(4,128)S(1)}, f32[4,256,256]{1,2,0:T(8,128)S(1)}) fusion(pred[256,256]{0,1:T(8,128)(4,1)S(1)} %copy-done.19, pred[256,256]{0,1:T(8,128)(4,1)S(1)} %get-tuple-element.42, pred[256,256]{0,1:T(8,128)(4,1)S(1)} %get-tuple-element.41, ...), kind=kOutput, calls=%fused_computation.36 | convolution fusion | flops 69465088 | bytes 2895872 | tf_op jit(solution)/shard_map/thd,shd->hts/dot_general | solution.py:78
  58.6 1.2 convolution_bitcast_fusion.5
  59.8 0.6 convolution_bitcast_fusion.1
  60.5 1.4 convolution_bitcast_fusion.4
  61.9 1.4 fusion.55
  63.4 1.5 collective-permute-start.4
  65.0 0.2 convolution_bitcast_fusion.6
  65.2 0.2 fusion.6
  65.4 12.2 %collective-permute-done.4 = f32[2,4,128,128]{2,3,1,0:T(8,128)S(1)} collective-permute-done((f32[2,4,128,128]{2,3,1,0:T(8,128)S(1)}, f32[2,4,128,128]{2,3,1,0:T(8,128)S(1)}, u32[]{:S(2)}, u32[]{:S(2)}) %collective-permute-start.4) | collective-permute-done | bytes 524320 | tf_op jit(solution)/shard_map/ppermute | solution.py:10
  77.7 0.7 copy-done.17
  78.4 1.4 collective-permute-start.5
  79.8 0.6 copy-done.26
  80.4 0.8 copy.106
  81.2 3.3 %fusion = bf16[1,256,2048]{2,1,0:T(8,128)(2,1)} fusion(bf16[256,512]{0,1:T(8,128)(2,1)S(1)} %bitcast.171, bf16[512,2048]{0,1:T(8,128)(2,1)} %bitcast.166), kind=kOutput, calls=%fused_computation.2 | convolution fusion | flops 537395200 | bytes 3407872 | tf_op jit(solution)/shard_map/dot_general | solution.py:73
  84.6 28.0 %reduce-scatter.2.cloned.1.call-done = f32[256,512]{0,1:T(8,128)} async-done(((f32[2048,512]{0,1:T(8,128)}), f32[256,512]{0,1:T(8,128)}) %reduce-scatter.2.cloned.1.call-update) | async-done | bytes 524304 | tf_op jit(solution)/shard_map/reduce_scatter | solution.py:113
  112.6 1.0 fusion.45
  113.6 1.3 fusion.9
  114.9 0.8 copy.107
  115.8 0.2 fusion.8
  116.0 0.8 copy.108
  116.9 36.8 %all-reduce.2.cloned.1.call-done = f32[512,256]{1,0:T(8,128)} async-done(((f32[512,256]{1,0:T(8,128)}), f32[512,256]{1,0:T(8,128)}) %all-reduce.2.cloned.1.call-update) | async-done | bytes 524304 | tf_op jit(solution)/shard_map/psum | solution.py:121
  153.6 1.9 %copy.161 = f32[512,256]{1,0:T(8,128)} copy(f32[512,256]{1,0:T(8,128)} %all-reduce.2.cloned.1.call-done) | data formatting | bytes 1048576
  (76 shorter events, 1.5 us)
Async XLA Ops:
  7.2 39.9 %copy-start = (bf16[1,256,2048]{2,1,0:T(8,128)(2,1)S(1)}, bf16[1,256,2048]{2,1,0:T(8,128)(2,1)}, u32[]{:S(2)}) copy-start(bf16[1,256,2048]{2,1,0:T(8,128)(2,1)} %param.11) | copy-start | bytes 3145732
  7.2 4.3 %copy-start.18 = (bf16[1,256,512]{2,1,0:T(8,128)(2,1)S(1)}, bf16[1,256,512]{2,1,0:T(8,128)(2,1)}, u32[]{:S(2)}) copy-start(bf16[1,256,512]{2,1,0:T(8,128)(2,1)} %param.6) | copy-start | bytes 786436
  7.2 4.4 %copy-start.21 = (f32[1,6,4,256]{3,2,1,0:T(4,128)S(1)}, f32[1,6,4,256]{3,2,1,0:T(4,128)}, u32[]{:S(2)}) copy-start(f32[1,6,4,256]{3,2,1,0:T(4,128)} %param.9) | copy-start | bytes 73732
  7.2 35.7 %all-gather.3.cloned.1.call-start = ((), (), s32[]{:S(2)}) async-start(), calls=%async_computation.3 | async-start | bytes 2359296 | tf_op jit(solution)/shard_map/all_gather | solution.py:72
  7.9 104.6 %reduce-scatter.2.cloned.1.call-start = ((), (), s32[]{:S(2)}) async-start(), calls=%async_computation.1 | async-start | bytes 4718592 | tf_op jit(solution)/shard_map/reduce_scatter | solution.py:113
  9.0 5.4 %copy-start.2 = (bf16[256,4,128]{2,1,0:T(4,128)(2,1)}, bf16[256,4,128]{2,1,0:T(4,128)(2,1)S(1)}, u32[]{:S(2)}) copy-start(bf16[256,4,128]{2,1,0:T(4,128)(2,1)S(1)} %reshape_squeeze.10) | copy-start | bytes 786436
  9.2 1.1 copy-start.12
  10.3 0.7 copy-start.4
  11.0 3.3 %collective-permute-start = (f32[4,128,128]{2,1,0:T(8,128)S(1)}, f32[4,128,128]{2,1,0:T(8,128)S(1)}, u32[]{:S(2)}, u32[]{:S(2)}) collective-permute-start(f32[4,128,128]{2,1,0:T(8,128)S(1)} %fusion.43), channel_id=1, source_target_pairs={{0,1},{1,0},{2,3},{3,2},{4,5},{5,4},{6,7},{7,6},{8,9},{9,8},{10,11... | collective-permute-start | bytes 786440 | tf_op jit(solution)/shard_map/ppermute | solution.py:10
  14.3 28.6 %copy-start.8 = (f32[4,128,128]{2,1,0:T(8,128)}, f32[4,128,128]{2,1,0:T(8,128)S(1)}, u32[]{:S(2)}) copy-start(f32[4,128,128]{2,1,0:T(8,128)S(1)} %collective-permute-done) | copy-start | bytes 786436
  14.4 11.6 %collective-permute-start.1 = (f32[4,128,128]{2,1,0:T(8,128)S(1)}, f32[4,128,128]{2,1,0:T(8,128)S(1)}, u32[]{:S(2)}, u32[]{:S(2)}) collective-permute-start(f32[4,128,128]{2,1,0:T(8,128)S(1)} %add.93), channel_id=1, source_target_pairs={{0,2},{1,3},{2,0},{3,1},{4,6},{5,7},{6,4},{7,5},{8,10},{9,11},{10,... | collective-permute-start | bytes 786440 | tf_op jit(solution)/shard_map/ppermute | solution.py:10
  26.0 16.9 %copy-start.6 = (f32[4,128,128]{2,1,0:T(8,128)}, f32[4,128,128]{2,1,0:T(8,128)S(1)}, u32[]{:S(2)}) copy-start(f32[4,128,128]{2,1,0:T(8,128)S(1)} %collective-permute-done.1) | copy-start | bytes 786436
  26.8 23.0 %collective-permute-start.2 = (f32[4,128,128]{2,1,0:T(8,128)}, f32[4,128,128]{2,1,0:T(8,128)}, u32[]{:S(2)}, u32[]{:S(2)}) collective-permute-start(f32[4,128,128]{2,1,0:T(8,128)} %add.95), channel_id=1, source_target_pairs={{0,4},{1,5},{2,6},{3,7},{4,0},{5,1},{6,2},{7,3},{8,12},{9,13},{10,... | collective-permute-start | bytes 786440 | tf_op jit(solution)/shard_map/ppermute | solution.py:10
  45.8 1.3 copy-start.1
  48.5 2.9 %copy-start.5 = (bf16[256,4,128]{2,1,0:T(4,128)(2,1)S(1)}, bf16[256,4,128]{2,1,0:T(4,128)(2,1)}, u32[]{:S(2)}) copy-start(bf16[256,4,128]{2,1,0:T(4,128)(2,1)} %copy-done.4) | copy-start | bytes 786436
  48.5 2.9 %copy-start.10 = (f32[256,4,128]{0,2,1:T(8,128)S(1)}, f32[256,4,128]{0,2,1:T(8,128)}, u32[]{:S(2)}) copy-start(f32[256,4,128]{0,2,1:T(8,128)} %convolution_bitcast_fusion.10) | copy-start | bytes 1572868
  48.5 2.9 %copy-start.11 = (f32[256,4,128]{0,2,1:T(8,128)S(1)}, f32[256,4,128]{0,2,1:T(8,128)}, u32[]{:S(2)}) copy-start(f32[256,4,128]{0,2,1:T(8,128)} %convolution_bitcast_fusion.9) | copy-start | bytes 1572868
  48.5 3.0 %copy-start.19 = (pred[256,256]{0,1:T(8,128)(4,1)S(1)}, pred[256,256]{0,1:T(8,128)(4,1)}, u32[]{:S(2)}) copy-start(pred[256,256]{0,1:T(8,128)(4,1)} %get-tuple-element.43) | copy-start | bytes 196612
  48.5 3.0 %copy-start.20 = (pred[256,256]{0,1:T(8,128)(4,1)S(1)}, pred[256,256]{0,1:T(8,128)(4,1)}, u32[]{:S(2)}) copy-start(pred[256,256]{0,1:T(8,128)(4,1)} %iota_compare_fusion) | copy-start | bytes 196612
  48.5 3.0 %copy-start.23 = (f32[256,4]{0,1:T(4,128)S(1)}, f32[256,4]{0,1:T(4,128)}, u32[]{:S(2)}) copy-start(f32[256,4]{0,1:T(4,128)} %get-tuple-element.36) | copy-start | bytes 12292
  48.6 3.0 %copy-start.24 = (f32[256,4]{0,1:T(4,128)S(1)}, f32[256,4]{0,1:T(4,128)}, u32[]{:S(2)}) copy-start(f32[256,4]{0,1:T(4,128)} %get-tuple-element.39) | copy-start | bytes 12292
  48.6 3.0 %copy-start.25 = (f32[256,4]{0,1:T(4,128)S(1)}, f32[256,4]{0,1:T(4,128)}, u32[]{:S(2)}) copy-start(f32[256,4]{0,1:T(4,128)} %get-tuple-element.40) | copy-start | bytes 12292
  49.8 1.8 %copy-start.14 = (f32[4,256,256]{1,2,0:T(8,128)S(1)}, f32[4,256,256]{1,2,0:T(8,128)}, u32[]{:S(2)}) copy-start(f32[4,256,256]{1,2,0:T(8,128)} %fusion.31) | copy-start | bytes 3145732
  54.9 0.7 copy-start.22
  54.9 98.7 %all-reduce.2.cloned.1.call-start = ((), (), s32[]{:S(2)}) async-start(), calls=%async_computation.2 | async-start | bytes 1048576 | tf_op jit(solution)/shard_map/psum | solution.py:121
  56.3 3.4 %copy-start.13 = (bf16[256,4,128]{0,2,1:T(8,128)(2,1)S(1)}, bf16[256,4,128]{0,2,1:T(8,128)(2,1)}, u32[]{:S(2)}) copy-start(bf16[256,4,128]{0,2,1:T(8,128)(2,1)} %copy-done.12) | copy-start | bytes 786436
  56.4 7.0 %collective-permute-start.3 = (f32[3,4,128,128]{2,3,1,0:T(8,128)S(1)}, f32[3,4,128,128]{2,3,1,0:T(8,128)S(1)}, u32[]{:S(2)}, u32[]{:S(2)}) collective-permute-start(f32[3,4,128,128]{2,3,1,0:T(8,128)S(1)} %pad_maximum_fusion), channel_id=1, source_target_pairs={{0,1},{1,0},{2,3},{3,2},{4,5},{5,4},{6,7},{7,6},{8,9},{9,8},{10,11... | collective-permute-start | bytes 2359304 | tf_op jit(solution)/shard_map/ppermute | solution.py:10
  60.4 1.5 copy-start.15
  63.3 1.6 %copy-start.7 = (f32[4,128,128]{2,1,0:T(8,128)S(1)}, f32[4,128,128]{2,1,0:T(8,128)}, u32[]{:S(2)}) copy-start(f32[4,128,128]{2,1,0:T(8,128)} %copy-done.6) | copy-start | bytes 786436
  63.3 1.8 %copy-start.9 = (f32[4,128,128]{2,1,0:T(8,128)S(1)}, f32[4,128,128]{2,1,0:T(8,128)}, u32[]{:S(2)}) copy-start(f32[4,128,128]{2,1,0:T(8,128)} %copy-done.8) | copy-start | bytes 786436
  63.4 14.2 %collective-permute-start.4 = (f32[2,4,128,128]{2,3,1,0:T(8,128)S(1)}, f32[2,4,128,128]{2,3,1,0:T(8,128)S(1)}, u32[]{:S(2)}, u32[]{:S(2)}) collective-permute-start(f32[2,4,128,128]{2,3,1,0:T(8,128)S(1)} %pad_maximum_fusion.1), channel_id=1, source_target_pairs={{0,2},{1,3},{2,0},{3,1},{4,6},{5,7},{6,4},{7,5},{8,10},{9,11},{10,... | collective-permute-start | bytes 1572872 | tf_op jit(solution)/shard_map/ppermute | solution.py:10
  77.6 0.8 copy-start.17
  78.4 34.2 %collective-permute-start.5 = (f32[1,4,128,128]{2,3,1,0:T(8,128)S(1)}, f32[1,4,128,128]{2,3,1,0:T(8,128)S(1)}, u32[]{:S(2)}, u32[]{:S(2)}) collective-permute-start(f32[1,4,128,128]{2,3,1,0:T(8,128)S(1)} %fusion.20), channel_id=1, source_target_pairs={{0,4},{1,5},{2,6},{3,7},{4,0},{5,1},{6,2},{7,3},{8,12},{9,13},{10,... | collective-permute-start | bytes 786440 | tf_op jit(solution)/shard_map/ppermute | solution.py:10
  79.8 0.6 copy-start.26
  84.6 31.2 %copy-start.3 = (bf16[256,4,128]{2,1,0:T(4,128)(2,1)S(1)}, bf16[256,4,128]{2,1,0:T(4,128)(2,1)}, u32[]{:S(2)}) copy-start(bf16[256,4,128]{2,1,0:T(4,128)(2,1)} %copy-done.2) | copy-start | bytes 786436
  84.6 31.2 %copy-start.16 = (f32[4,128,256]{2,1,0:T(8,128)S(1)}, f32[4,128,256]{2,1,0:T(8,128)}, u32[]{:S(2)}) copy-start(f32[4,128,256]{2,1,0:T(8,128)} %fusion.55) | copy-start | bytes 1572868
Sparse Core Ops, SparseCore 0:
  9.9 32.9 all-gather.2
  55.0 57.5 reduce-scatter.1
  114.9 38.6 all-reduce.1
